TPU v7x, 256 devices: a whole 4x4x8 slice. The times are simulated.
256 devices in a mesh: row: 16 (over y, x), col: 8 (over z), rep: 2 (over core).
Axes of the slice: x: 4, y: 4, z: 8, core: 2. Of those that a mesh axis runs over, the one named last changes fastest.
Arguments:
- patches: bfloat16 [2, 512, 6144], P('rep', 'col', 'row'), may hold values from -6 to 6
- cotangent: bfloat16 [2, 512, 6144], P('rep', 'col', 'row'), may hold values from -6 to 6
- w_in: bfloat16 [6144, 24576], P('row', 'col'), may hold values from -0.078125 to 0.078125
- w_out: bfloat16 [24576, 6144], P('col', 'row'), may hold values from -0.0390625 to 0.0390625
- moment_in: bfloat16 [2, 6144, 24576], P('rep', 'row', 'col'), may hold values from -2 to 2
- moment_out: bfloat16 [2, 24576, 6144], P('rep', 'col', 'row'), may hold values from -2 to 2
Outputs:
- mixed: bfloat16 [2, 512, 6144], P('rep', 'col', 'row')
- tally_in: bfloat16 [6144, 24576], P('row', 'col')
- tally_out: bfloat16 [24576, 6144], P('col', 'row')
All inputs are finite; a program needn't handle non-finite values.
Results may differ from a plain program's by a relative error of at most 0.0055.
Values may be sent and summed in bfloat16 or wider, within the bound.
A program may use at most 128 MiB of HBM per device.

v0:
```python
import math

import jax
import jax.numpy as jnp
from jax import lax
from jax.sharding import PartitionSpec as P

momentum_decay = 0.9
vote_scale = 0.3


def joined_along(blocks, dim):
    blocks = jnp.moveaxis(blocks, 0, dim)
    lengths = blocks.shape
    return blocks.reshape(*lengths[:dim], lengths[dim] * lengths[dim + 1], *lengths[dim + 2 :])


def sent_to_all(value, axis):
    copies = jnp.broadcast_to(value, (lax.axis_size(axis), *value.shape))
    return lax.all_to_all(copies, axis, split_axis=0, concat_axis=0, tiled=True)


def gather_directly(value, axis, dim):
    return joined_along(sent_to_all(value, axis), dim)


def cut_along(value, dim, peers):
    before, after = (value.shape[:dim], value.shape[dim + 1 :])
    return jnp.moveaxis(value.reshape(*before, peers, -1, *after), dim, 0)


def sum_at_owner(value, axis, dim):
    blocks = cut_along(value, dim, lax.axis_size(axis))
    arrived = lax.all_to_all(blocks, axis, split_axis=0, concat_axis=0, tiled=True)
    return arrived.sum(axis=0)


def gelu_value(pre):
    return 0.5 * pre * (1.0 + lax.erf(pre * (1.0 / math.sqrt(2.0))))


def gelu_slope(pre):
    return 0.5 * (1.0 + lax.erf(pre * (1.0 / math.sqrt(2.0)))) + pre * jnp.exp(-0.5 * pre * pre) * (
        1.0 / math.sqrt(2.0 * math.pi)
    )


def shards(patches, cotangent, w_in, w_out, moment_in, moment_out):
    inputs = gather_directly(patches[0], "col", 0)
    total_rows = inputs.shape[0]
    norm_factor = 1.0 / math.sqrt(total_rows)
    pre_whole = lax.psum(jnp.dot(inputs, w_in, preferred_element_type=jnp.float32), "row")
    hidden = gelu_value(pre_whole).astype(jnp.bfloat16)
    block = hidden
    mixed = sum_at_owner(
        jnp.dot(block, w_out, preferred_element_type=jnp.float32), "col", 0
    ).astype(jnp.bfloat16)
    grads = lax.all_gather(cotangent[0], "col", axis=0, tiled=True)
    block = grads
    back_whole = lax.psum(
        lax.dot_general(
            block, w_out, (((1,), (1,)), ((), ())), preferred_element_type=jnp.float32
        ).astype(jnp.bfloat16),
        "row",
    ).astype(jnp.float32)
    slope = (back_whole * gelu_slope(pre_whole)).astype(jnp.bfloat16)
    grad_first = (
        lax.dot_general(inputs, slope, (((0,), (0,)), ((), ())), preferred_element_type=jnp.float32)
        * norm_factor
    )
    grad_second = (
        lax.dot_general(hidden, grads, (((0,), (0,)), ((), ())), preferred_element_type=jnp.float32)
        * norm_factor
    )
    moved_first = (
        momentum_decay * moment_in[0].astype(jnp.float32) + (1.0 - momentum_decay) * grad_first
    )
    moved_second = (
        momentum_decay * moment_out[0].astype(jnp.float32) + (1.0 - momentum_decay) * grad_second
    )
    vote_first = jnp.tanh(moved_first / vote_scale).astype(jnp.bfloat16)
    vote_second = jnp.tanh(moved_second / vote_scale).astype(jnp.bfloat16)
    tally_first, tally_second = (
        lax.psum(vote_first, "rep").astype(jnp.float32),
        lax.psum(vote_second, "rep").astype(jnp.float32),
    )
    return (mixed[None], tally_first.astype(jnp.bfloat16), tally_second.astype(jnp.bfloat16))


def solution(mesh):
    in_specs = (
        P("rep", "col", "row"),
        P("rep", "col", "row"),
        P("row", "col"),
        P("col", "row"),
        P("rep", "row", "col"),
        P("rep", "col", "row"),
    )
    out_specs = (P("rep", "col", "row"), P("row", "col"), P("col", "row"))
    return jax.shard_map(shards, mesh=mesh, in_specs=in_specs, out_specs=out_specs, check_vma=False)
```

profile of v0, /device:TPU:1, one launch (start us, length us, event | category | flops | bytes accessed | tf_op | source)
XLA Modules:
  0.0 338.2 jit_solution(2649844550422343762)
XLA Ops:
  7.2 0.0 copy-start
  7.2 0.0 all-reduce.5.cloned.1.call-start
  7.2 1.0 broadcast_in_dim.4
  8.2 22.4 %all_to_all.10 = bf16[8,64,384]{2,1,0:T(8,128)(2,1)S(1)} all-to-all(bf16[8,64,384]{2,1,0:T(8,128)(2,1)S(1)} %broadcast_in_dim.4), channel_id=1, replica_groups=mesh['row'=16,'col'=8,'rep'=2] {'col'}, dimensions={0} | all-to-all | bytes 786432 | tf_op jit(solution)/shard_map/all_to_all | solution.py:20
  30.6 6.1 %fusion.20 = f32[512,3072]{1,0:T(8,128)} fusion(bf16[512,384]{1,0:T(8,128)(2,1)S(1)} %bitcast.36, bf16[384,3072]{1,0:T(8,128)(2,1)} %param.8), kind=kOutput, calls=%fused_computation.26 | convolution fusion | flops 1207959552 | bytes 9043968 | tf_op jit(solution)/shard_map/dot_general | solution.py:52
  36.7 0.0 copy-start.2
  36.7 0.0 all-reduce.5.cloned.1.call-update
  36.7 0.0 all-reduce.7.cloned.1.call-start
  36.8 0.7 copy-done.2
  37.5 20.5 %all-gather = bf16[1,512,384]{2,1,0:T(8,128)(2,1)S(1)} all-gather(bf16[1,64,384]{2,1,0:T(8,128)(2,1)S(1)} %copy-done.2), channel_id=2, replica_groups=mesh['row'=16,'col'=8,'rep'=2] {'col'}, dimensions={1}, use_global_device_ids=true | all-gather | bytes 442368 | tf_op jit(solution)/shard_map/all_gather | solution.py:58
  58.0 0.0 copy-done
  58.0 3.5 %convolution_convert_fusion = bf16[512,3072]{1,0:T(8,128)(2,1)} fusion(bf16[3072,384]{1,0:T(8,128)(2,1)S(1)} %copy-done, bf16[1,512,384]{2,1,0:T(8,128)(2,1)S(1)} %all-gather), kind=kOutput, calls=%fused_computation.17 | convolution fusion | flops 1209532416 | bytes 5898240 | tf_op jit(solution)/shard_map/dot_general | solution.py:61
  61.4 0.0 all-reduce.7.cloned.1.call-update
  61.5 0.0 all-reduce.9.cloned.1.call-start
  61.5 4.3 %copy.9 = bf16[1,384,3072]{1,2,0:T(8,128)(2,1)} copy(bf16[1,384,3072]{2,1,0:T(8,128)(2,1)} %param.10) | data formatting | bytes 4718592 | tf_op args[4]
  65.8 101.0 %all-reduce.5.cloned.1.call-done = f32[512,3072]{1,0:T(8,128)} async-done(((f32[512,3072]{1,0:T(8,128)}), f32[512,3072]{1,0:T(8,128)}) %all-reduce.5.cloned.1.call-update) | async-done | bytes 6291472 | tf_op jit(solution)/shard_map/psum | solution.py:52
  166.8 0.0 copy-start.3
  166.8 3.6 %multiply_convert_fusion = bf16[512,3072]{1,0:T(8,128)(2,1)S(1)} fusion(f32[512,3072]{1,0:T(8,128)} %all-reduce.5.cloned.1.call-done), kind=kLoop, calls=%fused_computation.7 | loop fusion | flops 7864320 | bytes 9437184 | tf_op jit(solution)/shard_map/convert_element_type | solution.py:53
  170.4 0.0 copy-start.1
  170.4 1.7 copy-done.1
  172.1 0.0 copy-done.3
  172.1 4.0 %fusion.8 = bf16[3072,384]{1,0:T(8,128)(2,1)} fusion(bf16[1,3072,384]{2,1,0:T(8,128)(2,1)S(1)} %copy-done.3, bf16[512,3072]{1,0:T(8,128)(2,1)S(1)} %multiply_convert_fusion, bf16[1,512,384]{2,1,0:T(8,128)(2,1)S(1)} %all-gather), kind=kOutput, calls=%fused_computation.12 | convolution fusion | flops 1215037440 | bytes 8257536 | tf_op jit(solution)/shard_map/dot_general | solution.py:72
  176.1 99.6 %all-reduce.7.cloned.1.call-done = bf16[512,3072]{1,0:T(8,128)(2,1)} async-done(((bf16[512,3072]{1,0:T(8,128)(2,1)}), bf16[512,3072]{1,0:T(8,128)(2,1)}) %all-reduce.7.cloned.1.call-update) | async-done | bytes 3145744 | tf_op jit(solution)/shard_map/psum | solution.py:60
  275.7 8.4 %fusion.11 = bf16[384,3072]{0,1:T(8,128)(2,1)} fusion(bf16[1,384,3072]{1,2,0:T(8,128)(2,1)} %copy.9, bf16[512,384]{1,0:T(8,128)(2,1)S(1)} %bitcast.37, f32[512,3072]{1,0:T(8,128)} %all-reduce.5.cloned.1.call-done, bf16[512,3072]{1,0:T(8,128)(2,1)} %all-reduce.7.cloned.1.call-done), kind=kOutput, calls=%fused_computation.16 | convolution fusion | flops 1232338944 | bytes 14548992 | tf_op jit(solution)/shard_map/dot_general | solution.py:68
  284.1 0.0 all-reduce.9.cloned.1.call-update
  284.1 3.7 %fusion.21 = f32[512,384]{1,0:T(8,128)S(1)} fusion(bf16[512,3072]{1,0:T(8,128)(2,1)} %copy-done.1, bf16[3072,384]{1,0:T(8,128)(2,1)S(1)} %copy-done), kind=kOutput, calls=%fused_computation.27 | convolution fusion | flops 1207959552 | bytes 6291456 | tf_op jit(solution)/shard_map/dot_general | solution.py:56
  287.8 27.9 %all_to_all.11 = f32[8,64,384]{2,1,0:T(8,128)S(1)} all-to-all(f32[8,64,384]{2,1,0:T(8,128)S(1)} %bitcast.38), channel_id=1, replica_groups=mesh['row'=16,'col'=8,'rep'=2] {'col'}, dimensions={0} | all-to-all | bytes 1572864 | tf_op jit(solution)/shard_map/all_to_all | solution.py:34
  315.7 0.7 reduce_sum.9
  316.4 7.7 %all-reduce.9.cloned.1.call-done = (bf16[384,3072]{0,1:T(8,128)(2,1)}, bf16[3072,384]{1,0:T(8,128)(2,1)}) async-done(((bf16[384,3072]{0,1:T(8,128)(2,1)}, bf16[3072,384]{1,0:T(8,128)(2,1)}), (bf16[384,3072]{0,1:T(8,128)(2,1)}, bf16[3072,384]{1,0:T(8,128)(2,1)})) %all-reduce.9.cloned.1.call-update) | async-done | bytes 4718608 | tf_op jit(solution)/shard_map/psum | solution.py:84
  324.1 4.3 %copy.10 = bf16[384,3072]{1,0:T(8,128)(2,1)} copy(bf16[384,3072]{0,1:T(8,128)(2,1)} %get-tuple-element.6) | data formatting | bytes 4718592
  328.4 3.3 copy.15
Async XLA Ops:
  7.2 50.8 %copy-start = (bf16[3072,384]{1,0:T(8,128)(2,1)S(1)}, bf16[3072,384]{1,0:T(8,128)(2,1)}, u32[]{:S(2)}) copy-start(bf16[3072,384]{1,0:T(8,128)(2,1)} %param.9) | copy-start | bytes 7077892
  7.2 159.7 %all-reduce.5.cloned.1.call-start = ((), (), s32[]{:S(2)}) async-start(), calls=%async_computation.2 | async-start | bytes 12582912 | tf_op jit(solution)/shard_map/psum | solution.py:52
  36.7 0.8 copy-start.2
  36.7 239.0 %all-reduce.7.cloned.1.call-start = ((), (), s32[]{:S(2)}) async-start(), calls=%async_computation.3 | async-start | bytes 6291456 | tf_op jit(solution)/shard_map/psum | solution.py:60
  61.5 262.7 %all-reduce.9.cloned.1.call-start = ((), (), s32[]{:S(2)}) async-start(), calls=%async_computation.4 | async-start | bytes 9437184 | tf_op jit(solution)/shard_map/psum | solution.py:84
  166.8 5.3 %copy-start.3 = (bf16[1,3072,384]{2,1,0:T(8,128)(2,1)S(1)}, bf16[1,3072,384]{2,1,0:T(8,128)(2,1)}, u32[]{:S(2)}) copy-start(bf16[1,3072,384]{2,1,0:T(8,128)(2,1)} %param.11) | copy-start | bytes 7077892
  170.4 1.7 copy-start.1
Sparse Core Ops, SparseCore 0:
  36.9 129.9 all-reduce.4
  170.2 105.4 all-reduce.6
  284.2 39.8 all-reduce.8
where the time goes:
time: 339 us; the launch traced here: 338 us
  waiting for transfers between devices  208 us (61%)
  blocking collectives  70.8 us (21%)
  matrix products  25.6 us (8%)
  local copies, waits for them, and re-layouts  15.3 us (5%)
  between operations  13.8 us (4%)
  other arithmetic  4.23 us (1%)
    psum x1, waiting for transfers between devices, shards(): lax.psum(jnp.dot(inputs, w_in, preferred_element_type=jnp.float32), 'row')  101 us
    psum x1, waiting for transfers between devices, shards(): lax.psum(lax.dot_general(block, w_out, (((1,), (1,)), ((), ())), preferre...  99.6 us
    all_to_all x1, blocking collectives, sum_at_owner(): lax.all_to_all(blocks, axis, split_axis=0, concat_axis=0, tiled=True)  27.9 us
    all_to_all x1, blocking collectives, sent_to_all(): return lax.all_to_all(copies, axis, split_axis=0, concat_axis=0, tiled=True)  22.4 us
    all_gather x1, blocking collectives, shards(): grads = lax.all_gather(cotangent[0], 'col', axis=0, tiled=True)  20.5 us
    unnamed x11, local copies, waits for them, and re-layouts  14.3 us
    dot_general x1, matrix products, shards(): lax.dot_general(inputs, slope, (((0,), (0,)), ((), ())), preferred_elemen...  8.39 us
    psum x1, waiting for transfers between devices, shards(): lax.psum(vote_first, 'rep').astype(jnp.float32)  7.74 us
  transfers between devices with their start and end apart: 3, of which 3 were waited for; matrix products, arithmetic and copies ran while one was open for 6% of the time, Pallas kernels for 0%

commit v1 on v0

v1 whole, which is shorter than its diff:
```python
import math

import jax
import jax.numpy as jnp
from jax import lax
from jax.experimental import pallas as pl
from jax.experimental.pallas import tpu as pltpu
from jax.sharding import PartitionSpec as P

MESH = pl.DeviceIdType.MESH
BF16, F32 = jnp.bfloat16, jnp.float32

momentum_decay = 0.9
vote_scale = 0.3

BLOCKS, TOKENS, FEATURES, PIECES, WIDTH = 8, 64, 384, 8, 384
UNITS = 2 * BLOCKS
RING = 4
SUB = TOKENS // RING
STAGES = 9


def gelu_value(pre):
    return 0.5 * pre * (1.0 + lax.erf(pre * (1.0 / math.sqrt(2.0))))


def gelu_slope(pre):
    return 0.5 * (1.0 + lax.erf(pre * (1.0 / math.sqrt(2.0)))) + pre * jnp.exp(-0.5 * pre * pre) * (
        1.0 / math.sqrt(2.0 * math.pi)
    )


def token_offset(slot):
    return ((slot + 1) // 2) * ((slot % 2) * 2 - 1)


def step_kernel(
    pat_h, cot_h, win_h, wout_h, min_h, mout_h,
    mixed_o, tin_o, tout_o,
    xs, ws, mom, part, t1, r1, summed, t2, r2, pre_s, act, pat_t,
    mpart, mrecv, mown, mout_v, votes, vrecv,
    ld, ost, zsend, zrecv, rsend, rrecv, asend, arecv, msend, mrcv, vsend, vrcv,
):
    row, col, rep = lax.axis_index("row"), lax.axis_index("col"), lax.axis_index("rep")
    x, y = row % RING, row // RING
    a = x * (1 - rep) + y * rep
    b = y * (1 - rep) + x * rep

    def peer(a_to, b_to):
        x_to = a_to * (1 - rep) + b_to * rep
        y_to = b_to * (1 - rep) + a_to * rep
        return (y_to * RING + x_to, col, rep)

    ap, am, a2 = (a + 1) % RING, (a + 3) % RING, (a + 2) % RING
    bp, bm, b2 = (b + 1) % RING, (b + 3) % RING, (b + 2) % RING
    to_ap, to_am, to_bp, to_bm = peer(ap, b), peer(am, b), peer(a, bp), peer(a, bm)
    partner = (row, col, 1 - rep)

    def send(src, dst, send_sem, recv_sem, device):
        copy = pltpu.make_async_remote_copy(
            src_ref=src, dst_ref=dst, send_sem=send_sem, recv_sem=recv_sem,
            device_id=device, device_id_type=MESH,
        )
        copy.start()

    def arrived(ref, sem):
        pltpu.make_async_remote_copy(
            src_ref=ref, dst_ref=ref, send_sem=sem, recv_sem=sem, device_id=partner, device_id_type=MESH
        ).wait_recv()

    def departed(ref, sem):
        pltpu.make_async_remote_copy(
            src_ref=ref, dst_ref=ref, send_sem=sem, recv_sem=sem, device_id=partner, device_id_type=MESH
        ).wait_send()

    load_x = [
        pltpu.make_async_copy(pat_h.at[0], xs.at[0], ld.at[0]),
        pltpu.make_async_copy(cot_h.at[0], xs.at[BLOCKS], ld.at[1]),
    ]
    load_win = [
        pltpu.make_async_copy(win_h.at[:, pl.ds(p * WIDTH, WIDTH)], ws.at[p], ld.at[4 + p]) for p in range(PIECES)
    ]
    load_wout = pltpu.make_async_copy(wout_h, ws.at[pl.ds(PIECES, PIECES)], ld.at[2])
    load_mout = pltpu.make_async_copy(mout_h, mom.at[pl.ds(PIECES, PIECES)], ld.at[3])
    load_min = [
        pltpu.make_async_copy(min_h.at[0, :, pl.ds(p * WIDTH, WIDTH)], mom.at[p], ld.at[4 + PIECES + p])
        for p in range(PIECES)
    ]
    for copy in load_x + load_win + [load_wout]:
        copy.start()

    barrier = pltpu.get_barrier_semaphore()
    peers = [to_ap, to_am, to_bp, to_bm, partner] + [(row, (col + d) % BLOCKS, rep) for d in range(1, BLOCKS)]
    for device in peers:
        pl.semaphore_signal(barrier, inc=1, device_id=device, device_id_type=MESH)
    for copy in load_x + load_win:
        copy.wait()
    pl.semaphore_wait(barrier, len(peers))

    for base in (0, BLOCKS):
        for slot in range(1, BLOCKS):
            target = (row, (col - token_offset(slot) + BLOCKS) % BLOCKS, rep)
            send(xs.at[base], xs.at[base + slot], zsend.at[base + slot], zrecv.at[base + slot], target)

    load_wout.wait()
    for copy in load_min + [load_mout]:
        copy.start()

    def reduce_start(q):
        @pl.when(q % BLOCKS != 0)
        def _():
            arrived(xs.at[q], zrecv.at[q])

        tokens = xs[q]

        @pl.when(q < BLOCKS)
        def _():
            for p in range(PIECES):
                part[q, p] = jnp.dot(tokens, ws[p], preferred_element_type=F32).astype(BF16)

        @pl.when(q >= BLOCKS)
        def _():
            for p in range(PIECES):
                part[q, p] = lax.dot_general(
                    tokens, ws[PIECES + p], (((1,), (1,)), ((), ())), preferred_element_type=F32
                ).astype(BF16)

        send(part.at[q, 2 * a2], t1.at[q, 0], rsend.at[0, q], rrecv.at[0, q], to_ap)
        send(part.at[q, 2 * a2 + 1], t1.at[q, 1], rsend.at[0, q], rrecv.at[0, q], to_am)
        send(part.at[q, 2 * ap + 1], r1.at[q, 1], rsend.at[0, q], rrecv.at[1, q], to_ap)
        send(part.at[q, 2 * am], r1.at[q, 2], rsend.at[0, q], rrecv.at[1, q], to_am)

    def reduce_relay(q):
        arrived(t1.at[q], rrecv.at[0, q])
        part[q, 2 * ap] = (part[q, 2 * ap].astype(F32) + t1[q, 0].astype(F32)).astype(BF16)
        part[q, 2 * am + 1] = (part[q, 2 * am + 1].astype(F32) + t1[q, 1].astype(F32)).astype(BF16)
        send(part.at[q, 2 * ap], r1.at[q, 0], rsend.at[1, q], rrecv.at[1, q], to_ap)
        send(part.at[q, 2 * am + 1], r1.at[q, 3], rsend.at[1, q], rrecv.at[1, q], to_am)

    def second_start(q):
        arrived(r1.at[q], rrecv.at[1, q])
        for h in range(2):
            total = part[q, 2 * a + h].astype(F32) + r1[q, h].astype(F32) + r1[q, 2 + h].astype(F32)
            summed[q, h] = total.astype(BF16).reshape(RING, SUB, WIDTH)
        send(summed.at[q, 0, b2], t2.at[q, 0], rsend.at[2, q], rrecv.at[2, q], to_bp)
        send(summed.at[q, 1, b2], t2.at[q, 1], rsend.at[2, q], rrecv.at[2, q], to_bm)
        send(summed.at[q, 1, bp], r2.at[q, 1], rsend.at[2, q], rrecv.at[3, q], to_bp)
        send(summed.at[q, 0, bm], r2.at[q, 2], rsend.at[2, q], rrecv.at[3, q], to_bm)

    def second_relay(q):
        arrived(t2.at[q], rrecv.at[2, q])
        summed[q, 0, bp] = (summed[q, 0, bp].astype(F32) + t2[q, 0].astype(F32)).astype(BF16)
        summed[q, 1, bm] = (summed[q, 1, bm].astype(F32) + t2[q, 1].astype(F32)).astype(BF16)
        send(summed.at[q, 0, bp], r2.at[q, 0], rsend.at[3, q], rrecv.at[3, q], to_bp)
        send(summed.at[q, 1, bm], r2.at[q, 3], rsend.at[3, q], rrecv.at[3, q], to_bm)

    def activate(q):
        arrived(r2.at[q], rrecv.at[3, q])
        totals = [
            summed[q, h, b].astype(F32) + r2[q, h].astype(F32) + r2[q, 2 + h].astype(F32) for h in range(2)
        ]

        @pl.when(q < BLOCKS)
        def _():
            for h in range(2):
                pre_s[q, h] = totals[h]
                act[q, 2 * a + h, b] = gelu_value(totals[h]).astype(BF16)

        @pl.when(q >= BLOCKS)
        def _():
            for h in range(2):
                slope = gelu_slope(pre_s[q - BLOCKS, h])
                act[q, 2 * a + h, b] = (totals[h] * slope).astype(BF16)

        mine = act.at[q, pl.ds(2 * a, 2), b]
        send(mine, mine, asend.at[0, q], arecv.at[0, q], to_bp)
        send(mine, mine, asend.at[0, q], arecv.at[0, q], to_bm)

    def second_spread(q):
        arrived(part.at[q, 0], arecv.at[0, q])
        ahead, behind = act.at[q, 2 * a, bm], act.at[q, 2 * a + 1, bp]
        send(ahead, ahead, asend.at[1, q], arecv.at[1, q], to_bp)
        send(behind, behind, asend.at[1, q], arecv.at[1, q], to_bm)

    def first_spread(q):
        arrived(t2.at[q], arecv.at[1, q])
        mine = act.at[q, pl.ds(2 * a, 2)]
        send(mine, mine, asend.at[2, q], arecv.at[2, q], to_ap)
        send(mine, mine, asend.at[2, q], arecv.at[2, q], to_am)

    def first_relay(q):
        arrived(r1.at[q], arecv.at[2, q])
        ahead, behind = act.at[q, 2 * am], act.at[q, 2 * ap + 1]
        send(ahead, ahead, asend.at[3, q], arecv.at[3, q], to_ap)
        send(behind, behind, asend.at[3, q], arecv.at[3, q], to_am)

    def complete(q):
        arrived(t1.at[q], arecv.at[3, q])

        @pl.when(q < BLOCKS)
        def _():
            total = jnp.zeros((TOKENS, FEATURES), F32)
            for p in range(PIECES):
                total += jnp.dot(
                    act[q, p].reshape(TOKENS, WIDTH), ws[PIECES + p], preferred_element_type=F32
                )

            @pl.when(q == 0)
            def _():
                mown[...] = total

            @pl.when(q > 0)
            def _():
                mpart[q] = total.astype(BF16)
                target = (row, (col + token_offset(q) + BLOCKS) % BLOCKS, rep)
                send(mpart.at[q], mrecv.at[q], msend.at[q], mrcv.at[q], target)

    grad_factor = (1.0 - momentum_decay) / vote_scale / math.sqrt(BLOCKS * TOKENS)
    moment_factor = momentum_decay / vote_scale

    def vote(grad, index):
        moved = moment_factor * mom[index].astype(F32) + grad_factor * grad
        votes[index] = jnp.tanh(moved).astype(BF16)
        send(votes.at[index], vrecv.at[index], vsend.at[index], vrcv.at[index], partner)

    def vote_second(p):
        hidden = act[pl.ds(0, BLOCKS), p].reshape(BLOCKS * TOKENS, WIDTH)
        cotangent = xs[pl.ds(BLOCKS, BLOCKS)].reshape(BLOCKS * TOKENS, FEATURES)
        grad = lax.dot_general(hidden, cotangent, (((0,), (0,)), ((), ())), preferred_element_type=F32)
        vote(grad, PIECES + p)

    def vote_first(p):
        slope = act[pl.ds(BLOCKS, BLOCKS), p].reshape(BLOCKS * TOKENS, WIDTH)
        grad = jnp.dot(pat_t[...], slope, preferred_element_type=F32)
        vote(grad, p)

    def tally(index):
        arrived(vrecv.at[index], vrcv.at[index])
        vrecv[index] = (votes[index].astype(F32) + vrecv[index].astype(F32)).astype(BF16)

    stages = (
        reduce_start, reduce_relay, second_start, second_relay, activate,
        second_spread, first_spread, first_relay, complete,
    )

    def turn(i, carry):
        for lag, stage in enumerate(stages):

            @pl.when((i >= lag) & (i < UNITS + lag))
            def _(lag=lag, stage=stage):
                stage(i - lag)

        @pl.when(i == UNITS)
        def _():
            load_mout.wait()
            pat_t[...] = xs[pl.ds(0, BLOCKS)].reshape(BLOCKS * TOKENS, FEATURES).T

        @pl.when(i >= UNITS)
        def _():
            vote_second(i - UNITS)

        return carry

    lax.fori_loop(0, UNITS + STAGES - 1, turn, 0)

    for copy in load_min:
        copy.wait()

    def first_turn(p, carry):
        vote_first(p)
        return carry

    lax.fori_loop(0, PIECES, first_turn, 0)

    def second_out(p, carry):
        tally(PIECES + p)
        pltpu.make_async_copy(vrecv.at[PIECES + p], tout_o.at[p], ost.at[PIECES + p]).start()
        return carry

    lax.fori_loop(0, PIECES, second_out, 0)

    total = mown[...]
    for slot in range(1, BLOCKS):
        arrived(mrecv.at[slot], mrcv.at[slot])
        total += mrecv[slot].astype(F32)
    mout_v[...] = total.astype(BF16)
    store_mixed = pltpu.make_async_copy(mout_v, mixed_o.at[0], ld.at[0])
    store_mixed.start()

    for p in range(PIECES):
        tally(p)
        pltpu.make_async_copy(vrecv.at[p], tin_o.at[:, pl.ds(p * WIDTH, WIDTH)], ost.at[p]).start()

    def drain(q, carry):
        departed(part.at[q, pl.ds(0, 4)], rsend.at[0, q])
        departed(part.at[q, pl.ds(0, 2)], rsend.at[1, q])
        departed(summed.at[q, 0], rsend.at[2, q])
        departed(t2.at[q], rsend.at[3, q])
        departed(summed.at[q, 0], asend.at[0, q])
        departed(t2.at[q], asend.at[1, q])
        departed(part.at[q, pl.ds(0, 4)], asend.at[2, q])
        departed(part.at[q, pl.ds(0, 2)], asend.at[3, q])
        departed(votes.at[q], vsend.at[q])

        @pl.when(q % BLOCKS != 0)
        def _():
            departed(xs.at[q], zsend.at[q])

        return carry

    lax.fori_loop(0, UNITS, drain, 0)
    for slot in range(1, BLOCKS):
        departed(mpart.at[slot], msend.at[slot])
    store_mixed.wait()
    for p in range(PIECES):
        pltpu.make_async_copy(vrecv.at[PIECES + p], tout_o.at[p], ost.at[PIECES + p]).wait()
        pltpu.make_async_copy(vrecv.at[p], tin_o.at[:, pl.ds(p * WIDTH, WIDTH)], ost.at[p]).wait()


def shards(patches, cotangent, w_in, w_out, moment_in, moment_out):
    by_piece = (PIECES, WIDTH, FEATURES)
    anywhere = pl.BlockSpec(memory_space=pl.ANY)
    mixed, tally_first, tally_second = pl.pallas_call(
        step_kernel,
        out_shape=(
            jax.ShapeDtypeStruct((1, TOKENS, FEATURES), BF16),
            jax.ShapeDtypeStruct((FEATURES, PIECES * WIDTH), BF16),
            jax.ShapeDtypeStruct(by_piece, BF16),
        ),
        in_specs=[anywhere] * 6,
        out_specs=(anywhere,) * 3,
        scratch_shapes=[
            pltpu.VMEM((UNITS, TOKENS, FEATURES), BF16),
            pltpu.VMEM((UNITS, WIDTH, FEATURES), BF16),
            pltpu.VMEM((UNITS, WIDTH, FEATURES), BF16),
            pltpu.VMEM((UNITS, PIECES, TOKENS, WIDTH), BF16),
            pltpu.VMEM((UNITS, 2, TOKENS, WIDTH), BF16),
            pltpu.VMEM((UNITS, 4, TOKENS, WIDTH), BF16),
            pltpu.VMEM((UNITS, 2, RING, SUB, WIDTH), BF16),
            pltpu.VMEM((UNITS, 2, SUB, WIDTH), BF16),
            pltpu.VMEM((UNITS, 4, SUB, WIDTH), BF16),
            pltpu.VMEM((BLOCKS, 2, SUB, WIDTH), F32),
            pltpu.VMEM((UNITS, PIECES, RING, SUB, WIDTH), BF16),
            pltpu.VMEM((FEATURES, BLOCKS * TOKENS), BF16),
            pltpu.VMEM((BLOCKS, TOKENS, FEATURES), BF16),
            pltpu.VMEM((BLOCKS, TOKENS, FEATURES), BF16),
            pltpu.VMEM((TOKENS, FEATURES), F32),
            pltpu.VMEM((TOKENS, FEATURES), BF16),
            pltpu.VMEM((UNITS, WIDTH, FEATURES), BF16),
            pltpu.VMEM((UNITS, WIDTH, FEATURES), BF16),
            pltpu.SemaphoreType.DMA((4 + 2 * PIECES,)),
            pltpu.SemaphoreType.DMA((UNITS,)),
            pltpu.SemaphoreType.DMA((UNITS,)),
            pltpu.SemaphoreType.DMA((UNITS,)),
            pltpu.SemaphoreType.DMA((4, UNITS)),
            pltpu.SemaphoreType.DMA((4, UNITS)),
            pltpu.SemaphoreType.DMA((4, UNITS)),
            pltpu.SemaphoreType.DMA((4, UNITS)),
            pltpu.SemaphoreType.DMA((BLOCKS,)),
            pltpu.SemaphoreType.DMA((BLOCKS,)),
            pltpu.SemaphoreType.DMA((UNITS,)),
            pltpu.SemaphoreType.DMA((UNITS,)),
        ],
        compiler_params=pltpu.CompilerParams(
            collective_id=0, has_side_effects=True, vmem_limit_bytes=60 * 1024 * 1024
        ),
    )(
        patches, cotangent, w_in, w_out.reshape(by_piece), moment_in, moment_out[0].reshape(by_piece),
    )
    return mixed, tally_first, tally_second.reshape(PIECES * WIDTH, FEATURES)


def solution(mesh):
    in_specs = (
        P("rep", "col", "row"),
        P("rep", "col", "row"),
        P("row", "col"),
        P("col", "row"),
        P("rep", "row", "col"),
        P("rep", "col", "row"),
    )
    out_specs = (P("rep", "col", "row"), P("row", "col"), P("col", "row"))
    return jax.shard_map(shards, mesh=mesh, in_specs=in_specs, out_specs=out_specs, check_vma=False)
```

time: 339 us -> 116 us (0.34)
  waiting for transfers between devices: 208 us -> 0 us
  Pallas kernels: 0 us -> 109 us
  blocking collectives: 70.8 us -> 0 us
  matrix products: 25.6 us -> 0 us
  between operations: 13.8 us -> 0.64 us
  local copies, waits for them, and re-layouts: 15.3 us -> 6.2 us
  other arithmetic: 4.23 us -> 0 us
    psum x3 -> x0, waiting for transfers between devices: 208 us -> none  [the longest x1 101 us: shards(): lax.psum(jnp.dot(inputs, w_in, preferred_element_type=jnp.float32), 'row')]
    pallas_call x0 -> x1, Pallas kernels: none -> 109 us  [shards(): pl.pallas_call(step_kernel, out_shape=(jax.ShapeDtypeStruct((1, TOKENS, F...]
    all_to_all x2 -> x0, blocking collectives: 50.3 us -> none  [the longest x1 27.9 us: sum_at_owner(): lax.all_to_all(blocks, axis, split_axis=0, concat_axis=0, tiled=True)]
    dot_general x5 -> x0, matrix products: 25.6 us -> none  [the longest x1 8.39 us: shards(): lax.dot_general(inputs, slope, (((0,), (0,)), ((), ())), preferred_elemen...]
    all_gather x1 -> x0, blocking collectives: 20.5 us -> none  [shards(): grads = lax.all_gather(cotangent[0], 'col', axis=0, tiled=True)]
    unnamed x11 -> x5, local copies, waits for them, and re-layouts: 14.3 us -> 6.2 us
    convert_element_type x1 -> x0, other arithmetic: 3.57 us -> none  [shards(): hidden = gelu_value(pre_whole).astype(jnp.bfloat16)]
  transfers between devices with their start and end apart: 3 -> 0, of which waited for: 3 -> 0; matrix products, arithmetic and copies ran while one was open for 6% -> 0% of each run, Pallas kernels for 0% -> 0%
where the time goes in v1:
time: 116 us
  Pallas kernels  109 us (94%)
  local copies, waits for them, and re-layouts  6.2 us (5%)
    pallas_call x1, Pallas kernels, shards(): pl.pallas_call(step_kernel, out_shape=(jax.ShapeDtypeStruct((1, TOKENS, F...  109 us
    unnamed x5, local copies, waits for them, and re-layouts  6.2 us

profile of v1, /device:TPU:1, one launch (start us, length us, event | category | flops | bytes accessed | tf_op | source)
XLA Modules:
  0.0 116.2 jit_solution(1956480940802922016)
XLA Ops:
  0.6 109.4 %shard_map.85 = (bf16[1,64,384]{2,1,0:T(8,128)(2,1)}, bf16[384,3072]{1,0:T(8,128)(2,1)}, bf16[8,384,384]{2,1,0:T(8,128)(2,1)}) custom-call(bf16[1,64,384]{2,1,0:T(8,128)(2,1)} %pat_h.1, bf16[1,64,384]{2,1,0:T(8,128)(2,1)} %cot_h.1, bf16[384,3072]{1,0:T(8,128)(2,1)} %win_h.1, bf16[8,384,384]{2,1,0:T(8,128)(2,1)} %bitcast.4, bf16[1,384,3072]{2,1,0:T(8,128)(2,1)} %min_h.1, ...), custom_call_target="tpu_custom_call" | custom-call | tf_op jit(solution)/shard_map/pallas_call | solution.py:323
  110.0 1.4 %copy.12 = bf16[1,64,384]{2,1,0:T(8,128)(2,1)} copy(bf16[1,64,384]{2,1,0:T(8,128)(2,1)} %get-tuple-element.12) | data formatting | bytes 98304
  111.4 0.0 copy-start
  111.4 3.4 %copy.13 = bf16[384,3072]{1,0:T(8,128)(2,1)} copy(bf16[384,3072]{1,0:T(8,128)(2,1)} %get-tuple-element.13) | data formatting | bytes 4718592
  114.8 0.0 copy-done
  114.8 1.4 %copy.14 = bf16[3072,384]{1,0:T(8,128)(2,1)} copy(bf16[3072,384]{1,0:T(8,128)(2,1)S(1)} %bitcast.3) | data formatting | bytes 4718592
Async XLA Ops:
  111.4 3.4 %copy-start = (bf16[8,384,384]{2,1,0:T(8,128)(2,1)S(1)}, bf16[8,384,384]{2,1,0:T(8,128)(2,1)}, u32[]{:S(2)}) copy-start(bf16[8,384,384]{2,1,0:T(8,128)(2,1)} %get-tuple-element.8) | copy-start | bytes 7077892

commit v2 on v1

--- a/solution.py
+++ b/solution.py
@@ -17,7 +17,9 @@
 UNITS = 2 * BLOCKS
 RING = 4
 SUB = TOKENS // RING
-STAGES = 9
+STAGES, LAG = 9, 2
+VMEM_LIMIT = 52 * 1024 * 1024
+TURNS = UNITS + LAG * (STAGES - 1)
 
 
 def gelu_value(pre):
@@ -36,10 +38,10 @@
 
 def step_kernel(
     pat_h, cot_h, win_h, wout_h, min_h, mout_h,
-    mixed_o, tin_o, tout_o,
-    xs, ws, mom, part, t1, r1, summed, t2, r2, pre_s, act, pat_t,
-    mpart, mrecv, mown, mout_v, votes, vrecv,
-    ld, ost, zsend, zrecv, rsend, rrecv, asend, arecv, msend, mrcv, vsend, vrcv,
+    mixed_v, tallies,
+    xs, ws, mom, part, own, t1, r1, summed, total_s, t2, r2, pre_s, act, pat_t,
+    mpart, mrecv, votes,
+    ld, zsend, zrecv, rsend, rrecv, asend, arecv, msend, mrcv, vsend, vrcv,
 ):
     row, col, rep = lax.axis_index("row"), lax.axis_index("col"), lax.axis_index("rep")
     x, y = row % RING, row // RING
@@ -113,17 +115,28 @@
 
         tokens = xs[q]
 
+        def piece(p):
+            return jnp.dot(tokens, ws[p], preferred_element_type=F32)
+
+        def piece_back(p):
+            return lax.dot_general(
+                tokens, ws[PIECES + p], (((1,), (1,)), ((), ())), preferred_element_type=F32
+            )
+
+        def products(term):
+            for block in (a2, ap, am):
+                for h in range(2):
+                    part[q, 2 * block + h] = term(2 * block + h).astype(BF16)
+            for h in range(2):
+                own[q, h] = term(2 * a + h)
+
         @pl.when(q < BLOCKS)
         def _():
-            for p in range(PIECES):
-                part[q, p] = jnp.dot(tokens, ws[p], preferred_element_type=F32).astype(BF16)
+            products(piece)
 
         @pl.when(q >= BLOCKS)
         def _():
-            for p in range(PIECES):
-                part[q, p] = lax.dot_general(
-                    tokens, ws[PIECES + p], (((1,), (1,)), ((), ())), preferred_element_type=F32
-                ).astype(BF16)
+            products(piece_back)
 
         send(part.at[q, 2 * a2], t1.at[q, 0], rsend.at[0, q], rrecv.at[0, q], to_ap)
         send(part.at[q, 2 * a2 + 1], t1.at[q, 1], rsend.at[0, q], rrecv.at[0, q], to_am)
@@ -140,8 +153,10 @@
     def second_start(q):
         arrived(r1.at[q], rrecv.at[1, q])
         for h in range(2):
-            total = part[q, 2 * a + h].astype(F32) + r1[q, h].astype(F32) + r1[q, 2 + h].astype(F32)
-            summed[q, h] = total.astype(BF16).reshape(RING, SUB, WIDTH)
+            total = own[q, h] + r1[q, h].astype(F32) + r1[q, 2 + h].astype(F32)
+            total = total.reshape(RING, SUB, WIDTH)
+            total_s[q, h] = total
+            summed[q, h] = total.astype(BF16)
         send(summed.at[q, 0, b2], t2.at[q, 0], rsend.at[2, q], rrecv.at[2, q], to_bp)
         send(summed.at[q, 1, b2], t2.at[q, 1], rsend.at[2, q], rrecv.at[2, q], to_bm)
         send(summed.at[q, 1, bp], r2.at[q, 1], rsend.at[2, q], rrecv.at[3, q], to_bp)
@@ -157,7 +172,7 @@
     def activate(q):
         arrived(r2.at[q], rrecv.at[3, q])
         totals = [
-            summed[q, h, b].astype(F32) + r2[q, h].astype(F32) + r2[q, 2 + h].astype(F32) for h in range(2)
+            total_s[q, h, b] + r2[q, h].astype(F32) + r2[q, 2 + h].astype(F32) for h in range(2)
         ]
 
         @pl.when(q < BLOCKS)
@@ -205,13 +220,10 @@
                     act[q, p].reshape(TOKENS, WIDTH), ws[PIECES + p], preferred_element_type=F32
                 )
 
-            @pl.when(q == 0)
-            def _():
-                mown[...] = total
+            mpart[q] = total
 
             @pl.when(q > 0)
             def _():
-                mpart[q] = total.astype(BF16)
                 target = (row, (col + token_offset(q) + BLOCKS) % BLOCKS, rep)
                 send(mpart.at[q], mrecv.at[q], msend.at[q], mrcv.at[q], target)
 
@@ -221,7 +233,7 @@
     def vote(grad, index):
         moved = moment_factor * mom[index].astype(F32) + grad_factor * grad
         votes[index] = jnp.tanh(moved).astype(BF16)
-        send(votes.at[index], vrecv.at[index], vsend.at[index], vrcv.at[index], partner)
+        send(votes.at[index], tallies.at[index], vsend.at[index], vrcv.at[index], partner)
 
     def vote_second(p):
         hidden = act[pl.ds(0, BLOCKS), p].reshape(BLOCKS * TOKENS, WIDTH)
@@ -235,8 +247,8 @@
         vote(grad, p)
 
     def tally(index):
-        arrived(vrecv.at[index], vrcv.at[index])
-        vrecv[index] = (votes[index].astype(F32) + vrecv[index].astype(F32)).astype(BF16)
+        arrived(tallies.at[index], vrcv.at[index])
+        tallies[index] = (votes[index].astype(F32) + tallies[index].astype(F32)).astype(BF16)
 
     stages = (
         reduce_start, reduce_relay, second_start, second_relay, activate,
@@ -244,24 +256,25 @@
     )
 
     def turn(i, carry):
-        for lag, stage in enumerate(stages):
+        for place, stage in enumerate(stages):
+            lag = LAG * place
 
             @pl.when((i >= lag) & (i < UNITS + lag))
             def _(lag=lag, stage=stage):
                 stage(i - lag)
 
-        @pl.when(i == UNITS)
+        @pl.when(i == TURNS - BLOCKS)
         def _():
             load_mout.wait()
             pat_t[...] = xs[pl.ds(0, BLOCKS)].reshape(BLOCKS * TOKENS, FEATURES).T
 
-        @pl.when(i >= UNITS)
-        def _():
-            vote_second(i - UNITS)
+        @pl.when(i >= TURNS - BLOCKS)
+        def _():
+            vote_second(i - (TURNS - BLOCKS))
 
         return carry
 
-    lax.fori_loop(0, UNITS + STAGES - 1, turn, 0)
+    lax.fori_loop(0, TURNS, turn, 0)
 
     for copy in load_min:
         copy.wait()
@@ -272,24 +285,23 @@
 
     lax.fori_loop(0, PIECES, first_turn, 0)
 
-    def second_out(p, carry):
+    def second_tally(p, carry):
         tally(PIECES + p)
-        pltpu.make_async_copy(vrecv.at[PIECES + p], tout_o.at[p], ost.at[PIECES + p]).start()
         return carry
 
-    lax.fori_loop(0, PIECES, second_out, 0)
-
-    total = mown[...]
+    lax.fori_loop(0, PIECES, second_tally, 0)
+
+    total = mpart[0]
     for slot in range(1, BLOCKS):
         arrived(mrecv.at[slot], mrcv.at[slot])
-        total += mrecv[slot].astype(F32)
-    mout_v[...] = total.astype(BF16)
-    store_mixed = pltpu.make_async_copy(mout_v, mixed_o.at[0], ld.at[0])
-    store_mixed.start()
-
-    for p in range(PIECES):
+        total += mrecv[slot]
+    mixed_v[...] = total.astype(BF16)
+
+    def first_tally(p, carry):
         tally(p)
-        pltpu.make_async_copy(vrecv.at[p], tin_o.at[:, pl.ds(p * WIDTH, WIDTH)], ost.at[p]).start()
+        return carry
+
+    lax.fori_loop(0, PIECES, first_tally, 0)
 
     def drain(q, carry):
         departed(part.at[q, pl.ds(0, 4)], rsend.at[0, q])
@@ -311,45 +323,53 @@
     lax.fori_loop(0, UNITS, drain, 0)
     for slot in range(1, BLOCKS):
         departed(mpart.at[slot], msend.at[slot])
-    store_mixed.wait()
+
+
+def output_kernel(mixed_v, tallies, mixed_o, tin_o, tout_o, sems):
+    copies = [
+        pltpu.make_async_copy(mixed_v, mixed_o.at[0], sems.at[0]),
+        pltpu.make_async_copy(tallies.at[pl.ds(PIECES, PIECES)], tout_o, sems.at[1]),
+    ]
     for p in range(PIECES):
-        pltpu.make_async_copy(vrecv.at[PIECES + p], tout_o.at[p], ost.at[PIECES + p]).wait()
-        pltpu.make_async_copy(vrecv.at[p], tin_o.at[:, pl.ds(p * WIDTH, WIDTH)], ost.at[p]).wait()
+        columns = tin_o.at[:, pl.ds(p * WIDTH, WIDTH)]
+        copies.append(pltpu.make_async_copy(tallies.at[p], columns, sems.at[2 + p]))
+    for copy in copies:
+        copy.start()
+    for copy in copies:
+        copy.wait()
 
 
 def shards(patches, cotangent, w_in, w_out, moment_in, moment_out):
     by_piece = (PIECES, WIDTH, FEATURES)
     anywhere = pl.BlockSpec(memory_space=pl.ANY)
-    mixed, tally_first, tally_second = pl.pallas_call(
+    in_vmem = pl.BlockSpec(memory_space=pltpu.VMEM)
+    results = pl.pallas_call(
         step_kernel,
         out_shape=(
-            jax.ShapeDtypeStruct((1, TOKENS, FEATURES), BF16),
-            jax.ShapeDtypeStruct((FEATURES, PIECES * WIDTH), BF16),
-            jax.ShapeDtypeStruct(by_piece, BF16),
+            pltpu.VMEM((TOKENS, FEATURES), BF16),
+            pltpu.VMEM((UNITS, WIDTH, FEATURES), BF16),
         ),
         in_specs=[anywhere] * 6,
-        out_specs=(anywhere,) * 3,
+        out_specs=(in_vmem,) * 2,
         scratch_shapes=[
             pltpu.VMEM((UNITS, TOKENS, FEATURES), BF16),
             pltpu.VMEM((UNITS, WIDTH, FEATURES), BF16),
             pltpu.VMEM((UNITS, WIDTH, FEATURES), BF16),
             pltpu.VMEM((UNITS, PIECES, TOKENS, WIDTH), BF16),
+            pltpu.VMEM((UNITS, 2, TOKENS, WIDTH), F32),
             pltpu.VMEM((UNITS, 2, TOKENS, WIDTH), BF16),
             pltpu.VMEM((UNITS, 4, TOKENS, WIDTH), BF16),
             pltpu.VMEM((UNITS, 2, RING, SUB, WIDTH), BF16),
+            pltpu.VMEM((UNITS, 2, RING, SUB, WIDTH), F32),
             pltpu.VMEM((UNITS, 2, SUB, WIDTH), BF16),
             pltpu.VMEM((UNITS, 4, SUB, WIDTH), BF16),
             pltpu.VMEM((BLOCKS, 2, SUB, WIDTH), F32),
             pltpu.VMEM((UNITS, PIECES, RING, SUB, WIDTH), BF16),
             pltpu.VMEM((FEATURES, BLOCKS * TOKENS), BF16),
-            pltpu.VMEM((BLOCKS, TOKENS, FEATURES), BF16),
-            pltpu.VMEM((BLOCKS, TOKENS, FEATURES), BF16),
-            pltpu.VMEM((TOKENS, FEATURES), F32),
-            pltpu.VMEM((TOKENS, FEATURES), BF16),
-            pltpu.VMEM((UNITS, WIDTH, FEATURES), BF16),
+            pltpu.VMEM((BLOCKS, TOKENS, FEATURES), F32),
+            pltpu.VMEM((BLOCKS, TOKENS, FEATURES), F32),
             pltpu.VMEM((UNITS, WIDTH, FEATURES), BF16),
             pltpu.SemaphoreType.DMA((4 + 2 * PIECES,)),
-            pltpu.SemaphoreType.DMA((UNITS,)),
             pltpu.SemaphoreType.DMA((UNITS,)),
             pltpu.SemaphoreType.DMA((UNITS,)),
             pltpu.SemaphoreType.DMA((4, UNITS)),
@@ -362,11 +382,23 @@
             pltpu.SemaphoreType.DMA((UNITS,)),
         ],
         compiler_params=pltpu.CompilerParams(
-            collective_id=0, has_side_effects=True, vmem_limit_bytes=60 * 1024 * 1024
+            collective_id=0, has_side_effects=True, vmem_limit_bytes=VMEM_LIMIT
         ),
     )(
         patches, cotangent, w_in, w_out.reshape(by_piece), moment_in, moment_out[0].reshape(by_piece),
     )
+    mixed, tally_first, tally_second = pl.pallas_call(
+        output_kernel,
+        out_shape=(
+            jax.ShapeDtypeStruct((1, TOKENS, FEATURES), BF16),
+            jax.ShapeDtypeStruct((FEATURES, PIECES * WIDTH), BF16),
+            jax.ShapeDtypeStruct(by_piece, BF16),
+        ),
+        in_specs=[in_vmem] * 2,
+        out_specs=(anywhere,) * 3,
+        scratch_shapes=[pltpu.SemaphoreType.DMA((2 + PIECES,))],
+        compiler_params=pltpu.CompilerParams(vmem_limit_bytes=2**20),
+    )(*results)
     return mixed, tally_first, tally_second.reshape(PIECES * WIDTH, FEATURES)
 
 

time: 116 us -> 97.8 us (0.84)
  Pallas kernels: 109 us -> 97.1 us
  local copies, waits for them, and re-layouts: 6.2 us -> 0 us
    pallas_call x1 -> x2, Pallas kernels: 109 us -> 97.1 us  [the longest x1 94.8 us: shards(): pl.pallas_call(step_kernel, out_shape=(pltpu.VMEM((TOKENS, FEATURES), BF1...]
    unnamed x5 -> x0, local copies, waits for them, and re-layouts: 6.2 us -> none
where the time goes in v2:
time: 97.8 us; the launch traced here: 97.7 us
  Pallas kernels  97.1 us (99%)
    pallas_call x1, Pallas kernels, shards(): pl.pallas_call(step_kernel, out_shape=(pltpu.VMEM((TOKENS, FEATURES), BF1...  94.8 us
    pallas_call x1, Pallas kernels, shards(): pl.pallas_call(output_kernel, out_shape=(jax.ShapeDtypeStruct((1, TOKENS,...  2.28 us

profile of v2, /device:TPU:1, one launch (start us, length us, event | category | flops | bytes accessed | tf_op | source)
XLA Modules:
  0.0 97.7 jit_solution(4492627859025247739)
XLA Ops:
  0.6 94.8 %shard_map.85 = (bf16[64,384]{1,0:T(8,128)(2,1)S(1)}, bf16[16,384,384]{2,1,0:T(8,128)(2,1)S(1)}) custom-call(bf16[1,64,384]{2,1,0:T(8,128)(2,1)} %pat_h.1, bf16[1,64,384]{2,1,0:T(8,128)(2,1)} %cot_h.1, bf16[384,3072]{1,0:T(8,128)(2,1)} %win_h.1, bf16[8,384,384]{2,1,0:T(8,128)(2,1)} %bitcast.3, bf16[1,384,3072]{2,1,0:T(8,128)(2,1)} %min_h.1, ...), custom_call_target="tpu_custom_call" | custom-call | tf_op jit(solution)/shard_map/pallas_call | solution.py:346
  95.5 2.3 %shard_map.86 = (bf16[1,64,384]{2,1,0:T(8,128)(2,1)}, bf16[384,3072]{1,0:T(8,128)(2,1)}, bf16[8,384,384]{2,1,0:T(8,128)(2,1)}) custom-call(bf16[64,384]{1,0:T(8,128)(2,1)S(1)} %get-tuple-element.8.mixed_v, bf16[16,384,384]{2,1,0:T(8,128)(2,1)S(1)} %get-tuple-element.9.tallies), custom_call_target="tpu_custom_call" | custom-call | tf_op jit(solution)/shard_map/pallas_call | solution.py:390

commit v3 on v2

--- a/solution.py
+++ b/solution.py
@@ -17,9 +17,10 @@
 UNITS = 2 * BLOCKS
 RING = 4
 SUB = TOKENS // RING
-STAGES, LAG = 9, 2
+LAGS = (0, 2, 5, 7, 10, 12, 15, 19, 23)
 VMEM_LIMIT = 52 * 1024 * 1024
-TURNS = UNITS + LAG * (STAGES - 1)
+TURNS = UNITS + LAGS[-1]
+TALLY_TURNS = 5
 
 
 def gelu_value(pre):
@@ -32,6 +33,11 @@
     )
 
 
+def unit_at(place):
+    moved = jnp.where(place <= BLOCKS, place - 1, place)
+    return jnp.where(place == 0, 0, jnp.where(place == 1, BLOCKS, moved))
+
+
 def token_offset(slot):
     return ((slot + 1) // 2) * ((slot % 2) * 2 - 1)
 
@@ -39,7 +45,7 @@
 def step_kernel(
     pat_h, cot_h, win_h, wout_h, min_h, mout_h,
     mixed_v, tallies,
-    xs, ws, mom, part, own, t1, r1, summed, total_s, t2, r2, pre_s, act, pat_t,
+    xs, ws, mom, part, own, t1, r1, summed, total_s, t2, r2, pre_s, act, pat_t, hid_t,
     mpart, mrecv, votes,
     ld, zsend, zrecv, rsend, rrecv, asend, arecv, msend, mrcv, vsend, vrcv,
 ):
@@ -74,6 +80,22 @@
         pltpu.make_async_remote_copy(
             src_ref=ref, dst_ref=ref, send_sem=sem, recv_sem=sem, device_id=partner, device_id_type=MESH
         ).wait_send()
+
+    def products(q, second):
+        tokens = xs[q]
+        for block in (a2, ap, am, a):
+            if second:
+                pair = ws[pl.ds(PIECES + 2 * block, 2)].reshape(2 * WIDTH, FEATURES)
+                term = lax.dot_general(tokens, pair, (((1,), (1,)), ((), ())), preferred_element_type=F32)
+            else:
+                pair = jnp.concatenate([ws[2 * block], ws[2 * block + 1]], axis=1)
+                term = jnp.dot(tokens, pair, preferred_element_type=F32)
+            for h in range(2):
+                half = term[:, h * WIDTH : (h + 1) * WIDTH]
+                if block is a:
+                    own[q, h] = half
+                else:
+                    part[q, 2 * block + h] = half.astype(BF16)
 
     load_x = [
         pltpu.make_async_copy(pat_h.at[0], xs.at[0], ld.at[0]),
@@ -97,6 +119,7 @@
         pl.semaphore_signal(barrier, inc=1, device_id=device, device_id_type=MESH)
     for copy in load_x + load_win:
         copy.wait()
+    products(0, False)
     pl.semaphore_wait(barrier, len(peers))
 
     for base in (0, BLOCKS):
@@ -108,36 +131,20 @@
     for copy in load_min + [load_mout]:
         copy.start()
 
+    def prepare(q):
+        @pl.when(q % BLOCKS != 0)
+        def _():
+            arrived(xs.at[q], zrecv.at[q])
+
+        @pl.when(q < BLOCKS)
+        def _():
+            products(q, False)
+
+        @pl.when(q >= BLOCKS)
+        def _():
+            products(q, True)
+
     def reduce_start(q):
-        @pl.when(q % BLOCKS != 0)
-        def _():
-            arrived(xs.at[q], zrecv.at[q])
-
-        tokens = xs[q]
-
-        def piece(p):
-            return jnp.dot(tokens, ws[p], preferred_element_type=F32)
-
-        def piece_back(p):
-            return lax.dot_general(
-                tokens, ws[PIECES + p], (((1,), (1,)), ((), ())), preferred_element_type=F32
-            )
-
-        def products(term):
-            for block in (a2, ap, am):
-                for h in range(2):
-                    part[q, 2 * block + h] = term(2 * block + h).astype(BF16)
-            for h in range(2):
-                own[q, h] = term(2 * a + h)
-
-        @pl.when(q < BLOCKS)
-        def _():
-            products(piece)
-
-        @pl.when(q >= BLOCKS)
-        def _():
-            products(piece_back)
-
         send(part.at[q, 2 * a2], t1.at[q, 0], rsend.at[0, q], rrecv.at[0, q], to_ap)
         send(part.at[q, 2 * a2 + 1], t1.at[q, 1], rsend.at[0, q], rrecv.at[0, q], to_am)
         send(part.at[q, 2 * ap + 1], r1.at[q, 1], rsend.at[0, q], rrecv.at[1, q], to_ap)
@@ -199,17 +206,20 @@
 
     def first_spread(q):
         arrived(t2.at[q], arecv.at[1, q])
-        mine = act.at[q, pl.ds(2 * a, 2)]
-        send(mine, mine, asend.at[2, q], arecv.at[2, q], to_ap)
-        send(mine, mine, asend.at[2, q], arecv.at[2, q], to_am)
+        near, far = act.at[q, 2 * a], act.at[q, 2 * a + 1]
+        send(near, near, asend.at[2, q], arecv.at[2, q], to_ap)
+        send(far, far, asend.at[2, q], arecv.at[2, q], to_am)
+        send(far, far, asend.at[2, q], arecv.at[4, q], to_ap)
+        send(near, near, asend.at[2, q], arecv.at[4, q], to_am)
 
     def first_relay(q):
-        arrived(r1.at[q], arecv.at[2, q])
+        arrived(t1.at[q], arecv.at[2, q])
         ahead, behind = act.at[q, 2 * am], act.at[q, 2 * ap + 1]
         send(ahead, ahead, asend.at[3, q], arecv.at[3, q], to_ap)
         send(behind, behind, asend.at[3, q], arecv.at[3, q], to_am)
 
     def complete(q):
+        arrived(t1.at[q], arecv.at[4, q])
         arrived(t1.at[q], arecv.at[3, q])
 
         @pl.when(q < BLOCKS)
@@ -222,6 +232,12 @@
 
             mpart[q] = total
 
+            @pl.when(q % 2 == 1)
+            def _():
+                rows = pl.ds(pl.multiple_of((q - 1) * TOKENS, 2 * TOKENS), 2 * TOKENS)
+                for p in range(PIECES):
+                    hid_t[p, :, rows] = act[pl.ds(q - 1, 2), p].reshape(2 * TOKENS, WIDTH).T
+
             @pl.when(q > 0)
             def _():
                 target = (row, (col + token_offset(q) + BLOCKS) % BLOCKS, rep)
@@ -236,19 +252,19 @@
         send(votes.at[index], tallies.at[index], vsend.at[index], vrcv.at[index], partner)
 
     def vote_second(p):
-        hidden = act[pl.ds(0, BLOCKS), p].reshape(BLOCKS * TOKENS, WIDTH)
         cotangent = xs[pl.ds(BLOCKS, BLOCKS)].reshape(BLOCKS * TOKENS, FEATURES)
-        grad = lax.dot_general(hidden, cotangent, (((0,), (0,)), ((), ())), preferred_element_type=F32)
+        grad = jnp.dot(hid_t[p], cotangent, preferred_element_type=F32)
         vote(grad, PIECES + p)
 
-    def vote_first(p):
-        slope = act[pl.ds(BLOCKS, BLOCKS), p].reshape(BLOCKS * TOKENS, WIDTH)
-        grad = jnp.dot(pat_t[...], slope, preferred_element_type=F32)
-        vote(grad, p)
+    def vote_first(block):
+        pieces = [act[pl.ds(BLOCKS, BLOCKS), 2 * block + h].reshape(BLOCKS * TOKENS, WIDTH) for h in range(2)]
+        grad = jnp.dot(pat_t[...], jnp.concatenate(pieces, axis=1), preferred_element_type=F32)
+        for h in range(2):
+            vote(grad[:, h * WIDTH : (h + 1) * WIDTH], 2 * block + h)
 
     def tally(index):
         arrived(tallies.at[index], vrcv.at[index])
-        tallies[index] = (votes[index].astype(F32) + tallies[index].astype(F32)).astype(BF16)
+        tallies[index] = votes[index] + tallies[index]
 
     stages = (
         reduce_start, reduce_relay, second_start, second_relay, activate,
@@ -256,12 +272,15 @@
     )
 
     def turn(i, carry):
-        for place, stage in enumerate(stages):
-            lag = LAG * place
+        for lag, stage in zip(LAGS, stages):
 
             @pl.when((i >= lag) & (i < UNITS + lag))
             def _(lag=lag, stage=stage):
-                stage(i - lag)
+                stage(unit_at(i - lag))
+
+        @pl.when(i < UNITS - 1)
+        def _():
+            prepare(unit_at(i + 1))
 
         @pl.when(i == TURNS - BLOCKS)
         def _():
@@ -271,6 +290,10 @@
         @pl.when(i >= TURNS - BLOCKS)
         def _():
             vote_second(i - (TURNS - BLOCKS))
+
+        @pl.when(i >= TURNS - TALLY_TURNS)
+        def _():
+            tally(PIECES + i - (TURNS - TALLY_TURNS))
 
         return carry
 
@@ -283,13 +306,13 @@
         vote_first(p)
         return carry
 
-    lax.fori_loop(0, PIECES, first_turn, 0)
+    lax.fori_loop(0, PIECES // 2, first_turn, 0)
 
     def second_tally(p, carry):
         tally(PIECES + p)
         return carry
 
-    lax.fori_loop(0, PIECES, second_tally, 0)
+    lax.fori_loop(TALLY_TURNS, PIECES, second_tally, 0)
 
     total = mpart[0]
     for slot in range(1, BLOCKS):
@@ -366,6 +389,7 @@
             pltpu.VMEM((BLOCKS, 2, SUB, WIDTH), F32),
             pltpu.VMEM((UNITS, PIECES, RING, SUB, WIDTH), BF16),
             pltpu.VMEM((FEATURES, BLOCKS * TOKENS), BF16),
+            pltpu.VMEM((PIECES, WIDTH, BLOCKS * TOKENS), BF16),
             pltpu.VMEM((BLOCKS, TOKENS, FEATURES), F32),
             pltpu.VMEM((BLOCKS, TOKENS, FEATURES), F32),
             pltpu.VMEM((UNITS, WIDTH, FEATURES), BF16),
@@ -375,7 +399,7 @@
             pltpu.SemaphoreType.DMA((4, UNITS)),
             pltpu.SemaphoreType.DMA((4, UNITS)),
             pltpu.SemaphoreType.DMA((4, UNITS)),
-            pltpu.SemaphoreType.DMA((4, UNITS)),
+            pltpu.SemaphoreType.DMA((5, UNITS)),
             pltpu.SemaphoreType.DMA((BLOCKS,)),
             pltpu.SemaphoreType.DMA((BLOCKS,)),
             pltpu.SemaphoreType.DMA((UNITS,)),

time: 97.8 us -> 93.9 us (0.960)
  Pallas kernels: 97.1 us -> 93.2 us
    pallas_call x1, Pallas kernels: 94.8 us -> 90.9 us  [shards(): pl.pallas_call(step_kernel, out_shape=(pltpu.VMEM((TOKENS, FEATURES), BF1...]
where the time goes in v3:
time: 93.9 us; the launch traced here: 93.8 us
  Pallas kernels  93.2 us (99%)
    pallas_call x1, Pallas kernels, shards(): pl.pallas_call(step_kernel, out_shape=(pltpu.VMEM((TOKENS, FEATURES), BF1...  90.9 us
    pallas_call x1, Pallas kernels, shards(): pl.pallas_call(output_kernel, out_shape=(jax.ShapeDtypeStruct((1, TOKENS,...  2.28 us

profile of v3, /device:TPU:1, one launch (start us, length us, event | category | flops | bytes accessed | tf_op | source)
XLA Modules:
  0.0 93.8 jit_solution(6301208860213735485)
XLA Ops:
  0.6 90.9 %shard_map.85 = (bf16[64,384]{1,0:T(8,128)(2,1)S(1)}, bf16[16,384,384]{2,1,0:T(8,128)(2,1)S(1)}) custom-call(bf16[1,64,384]{2,1,0:T(8,128)(2,1)} %pat_h.1, bf16[1,64,384]{2,1,0:T(8,128)(2,1)} %cot_h.1, bf16[384,3072]{1,0:T(8,128)(2,1)} %win_h.1, bf16[8,384,384]{2,1,0:T(8,128)(2,1)} %bitcast.3, bf16[1,384,3072]{2,1,0:T(8,128)(2,1)} %min_h.1, ...), custom_call_target="tpu_custom_call" | custom-call | tf_op jit(solution)/shard_map/pallas_call | solution.py:369
  91.5 2.3 %shard_map.86 = (bf16[1,64,384]{2,1,0:T(8,128)(2,1)}, bf16[384,3072]{1,0:T(8,128)(2,1)}, bf16[8,384,384]{2,1,0:T(8,128)(2,1)}) custom-call(bf16[64,384]{1,0:T(8,128)(2,1)S(1)} %get-tuple-element.8.mixed_v, bf16[16,384,384]{2,1,0:T(8,128)(2,1)S(1)} %get-tuple-element.9.tallies), custom_call_target="tpu_custom_call" | custom-call | tf_op jit(solution)/shard_map/pallas_call | solution.py:414

commit v4 on v3

--- a/solution.py
+++ b/solution.py
@@ -18,9 +18,8 @@
 RING = 4
 SUB = TOKENS // RING
 LAGS = (0, 2, 5, 7, 10, 12, 15, 19, 23)
-VMEM_LIMIT = 52 * 1024 * 1024
+VMEM_LIMIT = 50 * 1024 * 1024
 TURNS = UNITS + LAGS[-1]
-TALLY_TURNS = 5
 
 
 def gelu_value(pre):
@@ -44,9 +43,9 @@
 
 def step_kernel(
     pat_h, cot_h, win_h, wout_h, min_h, mout_h,
-    mixed_v, tallies,
+    mixed_v, votes, theirs,
     xs, ws, mom, part, own, t1, r1, summed, total_s, t2, r2, pre_s, act, pat_t, hid_t,
-    mpart, mrecv, votes,
+    mpart, mrecv,
     ld, zsend, zrecv, rsend, rrecv, asend, arecv, msend, mrcv, vsend, vrcv,
 ):
     row, col, rep = lax.axis_index("row"), lax.axis_index("col"), lax.axis_index("rep")
@@ -114,7 +113,8 @@
         copy.start()
 
     barrier = pltpu.get_barrier_semaphore()
-    peers = [to_ap, to_am, to_bp, to_bm, partner] + [(row, (col + d) % BLOCKS, rep) for d in range(1, BLOCKS)]
+    below, above = (row, (col + BLOCKS - 1) % BLOCKS, rep), (row, (col + 1) % BLOCKS, rep)
+    peers = [to_ap, to_am, to_bp, to_bm, partner, below, above]
     for device in peers:
         pl.semaphore_signal(barrier, inc=1, device_id=device, device_id_type=MESH)
     for copy in load_x + load_win:
@@ -123,9 +123,8 @@
     pl.semaphore_wait(barrier, len(peers))
 
     for base in (0, BLOCKS):
-        for slot in range(1, BLOCKS):
-            target = (row, (col - token_offset(slot) + BLOCKS) % BLOCKS, rep)
-            send(xs.at[base], xs.at[base + slot], zsend.at[base + slot], zrecv.at[base + slot], target)
+        send(xs.at[base], xs.at[base + 1], zsend.at[base + 1], zrecv.at[base + 1], below)
+        send(xs.at[base], xs.at[base + 2], zsend.at[base + 2], zrecv.at[base + 2], above)
 
     load_wout.wait()
     for copy in load_min + [load_mout]:
@@ -135,6 +134,11 @@
         @pl.when(q % BLOCKS != 0)
         def _():
             arrived(xs.at[q], zrecv.at[q])
+
+        @pl.when((q % BLOCKS >= 1) & (q % BLOCKS < BLOCKS - 2))
+        def _():
+            onward = (row, (col + BLOCKS + 1 - 2 * (q % 2)) % BLOCKS, rep)
+            send(xs.at[q], xs.at[q + 2], zsend.at[q + 2], zrecv.at[q + 2], onward)
 
         @pl.when(q < BLOCKS)
         def _():
@@ -249,7 +253,7 @@
     def vote(grad, index):
         moved = moment_factor * mom[index].astype(F32) + grad_factor * grad
         votes[index] = jnp.tanh(moved).astype(BF16)
-        send(votes.at[index], tallies.at[index], vsend.at[index], vrcv.at[index], partner)
+        send(votes.at[index], theirs.at[index], vsend.at[index], vrcv.at[index], partner)
 
     def vote_second(p):
         cotangent = xs[pl.ds(BLOCKS, BLOCKS)].reshape(BLOCKS * TOKENS, FEATURES)
@@ -262,10 +266,6 @@
         for h in range(2):
             vote(grad[:, h * WIDTH : (h + 1) * WIDTH], 2 * block + h)
 
-    def tally(index):
-        arrived(tallies.at[index], vrcv.at[index])
-        tallies[index] = votes[index] + tallies[index]
-
     stages = (
         reduce_start, reduce_relay, second_start, second_relay, activate,
         second_spread, first_spread, first_relay, complete,
@@ -291,10 +291,6 @@
         def _():
             vote_second(i - (TURNS - BLOCKS))
 
-        @pl.when(i >= TURNS - TALLY_TURNS)
-        def _():
-            tally(PIECES + i - (TURNS - TALLY_TURNS))
-
         return carry
 
     lax.fori_loop(0, TURNS, turn, 0)
@@ -307,24 +303,12 @@
         return carry
 
     lax.fori_loop(0, PIECES // 2, first_turn, 0)
-
-    def second_tally(p, carry):
-        tally(PIECES + p)
-        return carry
-
-    lax.fori_loop(TALLY_TURNS, PIECES, second_tally, 0)
 
     total = mpart[0]
     for slot in range(1, BLOCKS):
         arrived(mrecv.at[slot], mrcv.at[slot])
         total += mrecv[slot]
     mixed_v[...] = total.astype(BF16)
-
-    def first_tally(p, carry):
-        tally(p)
-        return carry
-
-    lax.fori_loop(0, PIECES, first_tally, 0)
 
     def drain(q, carry):
         departed(part.at[q, pl.ds(0, 4)], rsend.at[0, q])
@@ -336,6 +320,7 @@
         departed(part.at[q, pl.ds(0, 4)], asend.at[2, q])
         departed(part.at[q, pl.ds(0, 2)], asend.at[3, q])
         departed(votes.at[q], vsend.at[q])
+        arrived(theirs.at[q], vrcv.at[q])
 
         @pl.when(q % BLOCKS != 0)
         def _():
@@ -348,16 +333,17 @@
         departed(mpart.at[slot], msend.at[slot])
 
 
-def output_kernel(mixed_v, tallies, mixed_o, tin_o, tout_o, sems):
-    copies = [
-        pltpu.make_async_copy(mixed_v, mixed_o.at[0], sems.at[0]),
-        pltpu.make_async_copy(tallies.at[pl.ds(PIECES, PIECES)], tout_o, sems.at[1]),
-    ]
-    for p in range(PIECES):
-        columns = tin_o.at[:, pl.ds(p * WIDTH, WIDTH)]
-        copies.append(pltpu.make_async_copy(tallies.at[p], columns, sems.at[2 + p]))
-    for copy in copies:
-        copy.start()
+def output_kernel(mixed_v, votes, theirs, mixed_o, tin_o, tout_o, tallies, sems):
+    copies = [pltpu.make_async_copy(mixed_v, mixed_o.at[0], sems.at[UNITS])]
+    copies[0].start()
+    for index in [*range(PIECES, UNITS), *range(PIECES)]:
+        tallies[index] = votes[index] + theirs[index]
+        if index < PIECES:
+            target = tin_o.at[:, pl.ds(index * WIDTH, WIDTH)]
+        else:
+            target = tout_o.at[index - PIECES]
+        copies.append(pltpu.make_async_copy(tallies.at[index], target, sems.at[index]))
+        copies[-1].start()
     for copy in copies:
         copy.wait()
 
@@ -371,9 +357,10 @@
         out_shape=(
             pltpu.VMEM((TOKENS, FEATURES), BF16),
             pltpu.VMEM((UNITS, WIDTH, FEATURES), BF16),
+            pltpu.VMEM((UNITS, WIDTH, FEATURES), BF16),
         ),
         in_specs=[anywhere] * 6,
-        out_specs=(in_vmem,) * 2,
+        out_specs=(in_vmem,) * 3,
         scratch_shapes=[
             pltpu.VMEM((UNITS, TOKENS, FEATURES), BF16),
             pltpu.VMEM((UNITS, WIDTH, FEATURES), BF16),
@@ -392,7 +379,6 @@
             pltpu.VMEM((PIECES, WIDTH, BLOCKS * TOKENS), BF16),
             pltpu.VMEM((BLOCKS, TOKENS, FEATURES), F32),
             pltpu.VMEM((BLOCKS, TOKENS, FEATURES), F32),
-            pltpu.VMEM((UNITS, WIDTH, FEATURES), BF16),
             pltpu.SemaphoreType.DMA((4 + 2 * PIECES,)),
             pltpu.SemaphoreType.DMA((UNITS,)),
             pltpu.SemaphoreType.DMA((UNITS,)),
@@ -418,10 +404,13 @@
             jax.ShapeDtypeStruct((FEATURES, PIECES * WIDTH), BF16),
             jax.ShapeDtypeStruct(by_piece, BF16),
         ),
-        in_specs=[in_vmem] * 2,
+        in_specs=[in_vmem] * 3,
         out_specs=(anywhere,) * 3,
-        scratch_shapes=[pltpu.SemaphoreType.DMA((2 + PIECES,))],
-        compiler_params=pltpu.CompilerParams(vmem_limit_bytes=2**20),
+        scratch_shapes=[
+            pltpu.VMEM((UNITS, WIDTH, FEATURES), BF16),
+            pltpu.SemaphoreType.DMA((UNITS + 1,)),
+        ],
+        compiler_params=pltpu.CompilerParams(vmem_limit_bytes=8 * 2**20),
     )(*results)
     return mixed, tally_first, tally_second.reshape(PIECES * WIDTH, FEATURES)
 

time: 93.9 us -> 90.3 us (0.962)
  Pallas kernels: 93.2 us -> 89.6 us
    pallas_call x1, Pallas kernels: 90.9 us -> 87.2 us  [shards(): pl.pallas_call(step_kernel, out_shape=(pltpu.VMEM((TOKENS, FEATURES), BF1...]
where the time goes in v4:
time: 90.3 us; the launch traced here: 90.2 us
  Pallas kernels  89.6 us (99%)
    pallas_call x1, Pallas kernels, shards(): pl.pallas_call(step_kernel, out_shape=(pltpu.VMEM((TOKENS, FEATURES), BF1...  87.2 us
    pallas_call x1, Pallas kernels, shards(): pl.pallas_call(output_kernel, out_shape=(jax.ShapeDtypeStruct((1, TOKENS,...  2.36 us

profile of v4, /device:TPU:1, one launch (start us, length us, event | category | flops | bytes accessed | tf_op | source)
XLA Modules:
  0.0 90.2 jit_solution(2708424613752621146)
XLA Ops:
  0.6 87.2 %shard_map.85 = (bf16[64,384]{1,0:T(8,128)(2,1)S(1)}, bf16[16,384,384]{2,1,0:T(8,128)(2,1)S(1)}, bf16[16,384,384]{2,1,0:T(8,128)(2,1)S(1)}) custom-call(bf16[1,64,384]{2,1,0:T(8,128)(2,1)} %pat_h.1, bf16[1,64,384]{2,1,0:T(8,128)(2,1)} %cot_h.1, bf16[384,3072]{1,0:T(8,128)(2,1)} %win_h.1, bf16[8,384,384]{2,1,0:T(8,128)(2,1)} %bitcast.3, ...), custom_call_target="tpu_custom_call" | custom-call | tf_op jit(solution)/shard_map/pallas_call | solution.py:355
  87.9 2.4 %shard_map.86 = (bf16[1,64,384]{2,1,0:T(8,128)(2,1)}, bf16[384,3072]{1,0:T(8,128)(2,1)}, bf16[8,384,384]{2,1,0:T(8,128)(2,1)}) custom-call(bf16[64,384]{1,0:T(8,128)(2,1)S(1)} %get-tuple-element.9.mixed_v, bf16[16,384,384]{2,1,0:T(8,128)(2,1)S(1)} %get-tuple-element.10.votes, bf16[16,384,384]{2,1,0:T(8,128)(2,1)S(1)} %get-tuple-element.11.theirs), custom_call_target="tpu_custom_call" | custom-call | tf_op jit(solution)/shard_map/pallas_call | solution.py:400

commit v5 on v4

--- a/solution.py
+++ b/solution.py
@@ -17,7 +17,7 @@
 UNITS = 2 * BLOCKS
 RING = 4
 SUB = TOKENS // RING
-LAGS = (0, 2, 5, 7, 10, 12, 15, 19, 23)
+LAGS = (0, 2, 5, 7, 10, 13, 16, 21, 26)
 VMEM_LIMIT = 50 * 1024 * 1024
 TURNS = UNITS + LAGS[-1]
 
@@ -109,14 +109,13 @@
         pltpu.make_async_copy(min_h.at[0, :, pl.ds(p * WIDTH, WIDTH)], mom.at[p], ld.at[4 + PIECES + p])
         for p in range(PIECES)
     ]
-    for copy in load_x + load_win + [load_wout]:
-        copy.start()
-
     barrier = pltpu.get_barrier_semaphore()
     below, above = (row, (col + BLOCKS - 1) % BLOCKS, rep), (row, (col + 1) % BLOCKS, rep)
     peers = [to_ap, to_am, to_bp, to_bm, partner, below, above]
     for device in peers:
         pl.semaphore_signal(barrier, inc=1, device_id=device, device_id_type=MESH)
+    for copy in load_x + load_win + [load_wout]:
+        copy.start()
     for copy in load_x + load_win:
         copy.wait()
     products(0, False)
@@ -267,12 +266,13 @@
             vote(grad[:, h * WIDTH : (h + 1) * WIDTH], 2 * block + h)
 
     stages = (
-        reduce_start, reduce_relay, second_start, second_relay, activate,
-        second_spread, first_spread, first_relay, complete,
+        (LAGS[0], reduce_start), (LAGS[1], reduce_relay), (LAGS[7], first_relay), (LAGS[6], first_spread),
+        (LAGS[2], second_start), (LAGS[3], second_relay), (LAGS[4], activate), (LAGS[5], second_spread),
+        (LAGS[8], complete),
     )
 
     def turn(i, carry):
-        for lag, stage in zip(LAGS, stages):
+        for lag, stage in stages:
 
             @pl.when((i >= lag) & (i < UNITS + lag))
             def _(lag=lag, stage=stage):
@@ -320,7 +320,6 @@
         departed(part.at[q, pl.ds(0, 4)], asend.at[2, q])
         departed(part.at[q, pl.ds(0, 2)], asend.at[3, q])
         departed(votes.at[q], vsend.at[q])
-        arrived(theirs.at[q], vrcv.at[q])
 
         @pl.when(q % BLOCKS != 0)
         def _():
@@ -331,6 +330,12 @@
     lax.fori_loop(0, UNITS, drain, 0)
     for slot in range(1, BLOCKS):
         departed(mpart.at[slot], msend.at[slot])
+
+    def theirs_in(q, carry):
+        arrived(theirs.at[UNITS - 1 - q], vrcv.at[UNITS - 1 - q])
+        return carry
+
+    lax.fori_loop(0, UNITS, theirs_in, 0)
 
 
 def output_kernel(mixed_v, votes, theirs, mixed_o, tin_o, tout_o, tallies, sems):

time: 90.3 us -> 89.2 us (0.988)
  Pallas kernels: 89.6 us -> 88.5 us
    pallas_call x1, Pallas kernels: 87.2 us -> 86.1 us  [shards(): pl.pallas_call(step_kernel, out_shape=(pltpu.VMEM((TOKENS, FEATURES), BF1...]
where the time goes in v5:
time: 89.2 us; the launch traced here: 89.1 us
  Pallas kernels  88.5 us (99%)
    pallas_call x1, Pallas kernels, shards(): pl.pallas_call(step_kernel, out_shape=(pltpu.VMEM((TOKENS, FEATURES), BF1...  86.1 us
    pallas_call x1, Pallas kernels, shards(): pl.pallas_call(output_kernel, out_shape=(jax.ShapeDtypeStruct((1, TOKENS,...  2.36 us

profile of v5, /device:TPU:1, one launch (start us, length us, event | category | flops | bytes accessed | tf_op | source)
XLA Modules:
  0.0 89.1 jit_solution(6764289893756856968)
XLA Ops:
  0.6 86.1 %shard_map.85 = (bf16[64,384]{1,0:T(8,128)(2,1)S(1)}, bf16[16,384,384]{2,1,0:T(8,128)(2,1)S(1)}, bf16[16,384,384]{2,1,0:T(8,128)(2,1)S(1)}) custom-call(bf16[1,64,384]{2,1,0:T(8,128)(2,1)} %pat_h.1, bf16[1,64,384]{2,1,0:T(8,128)(2,1)} %cot_h.1, bf16[384,3072]{1,0:T(8,128)(2,1)} %win_h.1, bf16[8,384,384]{2,1,0:T(8,128)(2,1)} %bitcast.3, ...), custom_call_target="tpu_custom_call" | custom-call | tf_op jit(solution)/shard_map/pallas_call | solution.py:360
  86.8 2.4 %shard_map.86 = (bf16[1,64,384]{2,1,0:T(8,128)(2,1)}, bf16[384,3072]{1,0:T(8,128)(2,1)}, bf16[8,384,384]{2,1,0:T(8,128)(2,1)}) custom-call(bf16[64,384]{1,0:T(8,128)(2,1)S(1)} %get-tuple-element.9.mixed_v, bf16[16,384,384]{2,1,0:T(8,128)(2,1)S(1)} %get-tuple-element.10.votes, bf16[16,384,384]{2,1,0:T(8,128)(2,1)S(1)} %get-tuple-element.11.theirs), custom_call_target="tpu_custom_call" | custom-call | tf_op jit(solution)/shard_map/pallas_call | solution.py:405

commit v6 on v5

--- a/solution.py
+++ b/solution.py
@@ -268,7 +268,6 @@
     stages = (
         (LAGS[0], reduce_start), (LAGS[1], reduce_relay), (LAGS[7], first_relay), (LAGS[6], first_spread),
         (LAGS[2], second_start), (LAGS[3], second_relay), (LAGS[4], activate), (LAGS[5], second_spread),
-        (LAGS[8], complete),
     )
 
     def turn(i, carry):
@@ -287,9 +286,17 @@
             load_mout.wait()
             pat_t[...] = xs[pl.ds(0, BLOCKS)].reshape(BLOCKS * TOKENS, FEATURES).T
 
-        @pl.when(i >= TURNS - BLOCKS)
-        def _():
-            vote_second(i - (TURNS - BLOCKS))
+        @pl.when(i > TURNS - BLOCKS)
+        def _():
+            vote_second(i - (TURNS - BLOCKS) - 1)
+
+        @pl.when(i == TURNS - 1)
+        def _():
+            vote_second(PIECES - 1)
+
+        @pl.when((i >= LAGS[8]) & (i < UNITS + LAGS[8]))
+        def _():
+            complete(unit_at(i - LAGS[8]))
 
         return carry
 

time: 89.2 us -> 88.9 us (level)
  no operation moved by 1% of the time
where the time goes in v6:
time: 88.9 us; the launch traced here: 88.8 us
  Pallas kernels  88.2 us (99%)
    pallas_call x1, Pallas kernels, shards(): pl.pallas_call(step_kernel, out_shape=(pltpu.VMEM((TOKENS, FEATURES), BF1...  85.8 us
    pallas_call x1, Pallas kernels, shards(): pl.pallas_call(output_kernel, out_shape=(jax.ShapeDtypeStruct((1, TOKENS,...  2.36 us

profile of v6, /device:TPU:1, one launch (start us, length us, event | category | flops | bytes accessed | tf_op | source)
XLA Modules:
  0.0 88.8 jit_solution(3734980055508491237)
XLA Ops:
  0.6 85.8 %shard_map.85 = (bf16[64,384]{1,0:T(8,128)(2,1)S(1)}, bf16[16,384,384]{2,1,0:T(8,128)(2,1)S(1)}, bf16[16,384,384]{2,1,0:T(8,128)(2,1)S(1)}) custom-call(bf16[1,64,384]{2,1,0:T(8,128)(2,1)} %pat_h.1, bf16[1,64,384]{2,1,0:T(8,128)(2,1)} %cot_h.1, bf16[384,3072]{1,0:T(8,128)(2,1)} %win_h.1, bf16[8,384,384]{2,1,0:T(8,128)(2,1)} %bitcast.3, ...), custom_call_target="tpu_custom_call" | custom-call | tf_op jit(solution)/shard_map/pallas_call | solution.py:367
  86.4 2.4 %shard_map.86 = (bf16[1,64,384]{2,1,0:T(8,128)(2,1)}, bf16[384,3072]{1,0:T(8,128)(2,1)}, bf16[8,384,384]{2,1,0:T(8,128)(2,1)}) custom-call(bf16[64,384]{1,0:T(8,128)(2,1)S(1)} %get-tuple-element.9.mixed_v, bf16[16,384,384]{2,1,0:T(8,128)(2,1)S(1)} %get-tuple-element.10.votes, bf16[16,384,384]{2,1,0:T(8,128)(2,1)S(1)} %get-tuple-element.11.theirs), custom_call_target="tpu_custom_call" | custom-call | tf_op jit(solution)/shard_map/pallas_call | solution.py:412
